TPU v7x, 128 devices: a whole 4x4x4 slice. The times are simulated.
128 devices in a mesh: row: 8 (over z_hi, y), col: 16 (over x, z_lo, core).
Axes of the slice: x: 4, y: 4, z: 4 (z_hi: 2, z_lo: 2; z = z_hi * 2 + z_lo), core: 2. Of those that a mesh axis runs over, the one named last changes fastest.
Arguments:
- student_hidden: bfloat16 [16384, 1920], P(('row', 'col')), may hold values from -6 to 6
- projection: bfloat16 [1920, 768], replicated, may hold values from -0.125 to 0.125
- teacher: bfloat16 [10240, 768], P(('row', 'col')), may hold values from -6 to 6
- block_map: int32 [128, 3, 4096], P(('row', 'col')), may hold values from 0 to 127, as said below
- block_counts: int32 [128, 128], P(('row', 'col')), may hold values from 16 to 32, as said below
- interp_weights: float32 [64], replicated, may hold values from 0.1 to 1
Outputs:
- grad_hidden: bfloat16 [16384, 1920], P(('row', 'col'))
Inputs may be any that keep to these rules, and one draw needn't show every extreme that they name: `block_map`: field 0 is a tubelet of the sending device below 80, field 1 a cell of the receiving device below 128, field 2 a level below 64. Slots to the sending device itself name cells near the tubelet's proportional position; slots to other devices name any of their cells. Dead slots hold values in range. `block_counts`: entry [s, d] counts the live slots from device s to device d, at the start of d's 32 slots; it is at least 16. In every draw some device receives 32 blocks from every device.
All inputs are finite; a program needn't handle non-finite values.
Results may differ from a plain program's by a relative error of at most 0.025.
Values may be sent and summed in bfloat16 or wider, within the bound.
A program may use at most 64 MiB of HBM per device.

v0:
```python
import jax
import jax.numpy as jnp
from jax import lax
from jax.sharding import Mesh
from jax.sharding import PartitionSpec as P

ROW_COL = ("row_0", "row_1", "col")
ROW = ("row_0", "row_1")


huber_delta = 0.05
norm_eps = 1e-06


def sent_together(arrays, axis, dim, along):
    both = jnp.concatenate(arrays, axis=along)
    whole, at, gathered = (lax.all_gather(both, axis, axis=dim, tiled=True), 0, [])
    for a in arrays:
        gathered.append(lax.slice_in_dim(whole, at, at + a.shape[along], axis=along))
        at += a.shape[along]
    return tuple(gathered)


def own_block(pieces, axes, turns):
    dims = [lax.axis_size(a) for a in axes]
    pieces = pieces.reshape(*dims, *pieces.shape[1:])
    pieces = pieces.transpose(*turns, *range(len(axes), pieces.ndim))
    pieces = pieces.reshape(-1, *pieces.shape[len(axes) :])
    for k in turns:
        pieces = lax.psum_scatter(pieces, axes[k], scatter_dimension=0, tiled=True)
    return pieces[0]


def split_up(array, dim, count):
    before, after = (array.shape[:dim], array.shape[dim + 1 :])
    return jnp.moveaxis(array.reshape(*before, count, -1, *after), dim, 0)


def summed_rows(array, axes, turns, dim):
    count = lax.axis_size(axes)
    return own_block(split_up(array, dim, count), axes, turns)


def local(student_hidden, projection, teacher, block_map, block_counts, interp_weights):
    slots = block_map.shape[2]
    peers = block_counts.shape[1]
    per_peer = slots // peers
    tokens_dev = student_hidden.shape[0]
    levels = interp_weights.shape[0]
    fields = block_map[0]
    tube_index = fields[0]
    cell_index = fields[1]
    level_index = fields[2]
    matches = level_index[:, None] == jnp.arange(levels, dtype=jnp.int32)[None, :]
    weights = jnp.sum(jnp.where(matches, interp_weights[None, :], 0.0), axis=1)
    live = (jnp.arange(per_peer, dtype=jnp.int32)[None, :] < block_counts[0][:, None]).reshape(
        slots
    )
    scale = weights * live.astype(jnp.float32)
    rows = teacher[tube_index]
    contrib = (rows.astype(jnp.float32) * scale[:, None]).astype(jnp.bfloat16)
    arrived, cells = (
        lax.all_to_all(contrib, ROW_COL, split_axis=0, concat_axis=0, tiled=True),
        lax.all_to_all(cell_index, ROW_COL, split_axis=0, concat_axis=0, tiled=True),
    )
    onehot = (cells[None, :] == jnp.arange(tokens_dev, dtype=jnp.int32)[:, None]).astype(
        jnp.bfloat16
    )
    target = jnp.dot(onehot, arrived, preferred_element_type=jnp.float32)
    teacher_unit = (
        target * lax.rsqrt(jnp.sum(target * target, axis=1, keepdims=True) + norm_eps)
    ).astype(jnp.bfloat16)
    proj = jnp.dot(student_hidden, projection, preferred_element_type=jnp.float32)
    inverse = lax.rsqrt(jnp.sum(proj * proj, axis=1, keepdims=True) + norm_eps)
    unit = proj * inverse
    student_unit = unit.astype(jnp.bfloat16)
    row_student, row_teacher = sent_together((student_unit, teacher_unit), "col", 0, 1)
    column_student, column_teacher = sent_together((student_unit, teacher_unit), ROW, 0, 1)
    contract = (((1,), (1,)), ((), ()))
    gram_s = lax.dot_general(
        row_student, column_student, contract, preferred_element_type=jnp.float32
    )
    gram_t = lax.dot_general(
        row_teacher, column_teacher, contract, preferred_element_type=jnp.float32
    )
    slope = jnp.clip((gram_s - gram_t) / huber_delta, -1.0, 1.0).astype(jnp.bfloat16)
    grad_unit = 2.0 * summed_rows(
        lax.dot_general(
            slope, row_student, (((0,), (0,)), ((), ())), preferred_element_type=jnp.float32
        ).astype(jnp.bfloat16),
        ROW,
        (1, 0),
        0,
    ).astype(jnp.float32)
    along = jnp.sum(unit * grad_unit, axis=1, keepdims=True)
    grad_proj = ((grad_unit - unit * along) * inverse).astype(jnp.bfloat16)
    grad_hidden = lax.dot_general(
        grad_proj, projection, contract, preferred_element_type=jnp.float32
    )
    return grad_hidden.astype(jnp.bfloat16)


def solution(mesh):
    split = Mesh(mesh.devices.reshape(2, 4, mesh.shape["col"]), ("row_0", "row_1", "col"))
    return jax.shard_map(
        local,
        mesh=split,
        in_specs=(
            P(ROW_COL, None),
            P(),
            P(ROW_COL, None),
            P(ROW_COL, None, None),
            P(ROW_COL, None),
            P(),
        ),
        out_specs=P(ROW_COL, None),
        check_vma=False,
    )
```

profile of v0, /device:TPU:1, one launch (start us, length us, event | category | flops | bytes accessed | tf_op | source)
XLA Modules:
  0.0 332.7 jit_solution(3375694467733573282)
XLA Ops:
  6.5 0.0 copy-start
  6.5 0.0 copy-start.1
  6.5 0.9 slice_reduce_fusion
  7.5 0.7 all_to_all.12
  8.2 11.5 %all-to-all-start = ((s32[128,32,1]{1,2,0:T(1,128)}), s32[128,32,1]{1,2,0:T(1,128)S(1)}, u32[]{:S(2)}, u32[]{:S(2)}) async-start(s32[128,32,1]{1,2,0:T(1,128)} %bitcast), calls=%async_computation | async-start | bytes 131072 | tf_op jit(solution)/shard_map/all_to_all | solution.py:64
  19.7 0.7 compare_select_fusion
  20.4 0.9 select_reduce_fusion
  21.3 0.1 reduce_sum.40
  21.4 0.7 fusion.24
  22.2 0.0 copy-done.1
  22.2 17.9 %gather_fusion = bf16[4096,768]{1,0:T(8,128)(2,1)} fusion(bf16[80,768]{1,0:T(8,128)(2,1)S(1)} %copy-done.1, s32[4096]{0:T(1024)S(1)} %broadcast_clamp_fusion), kind=kCustom, calls=%fused_computation | custom fusion | bytes 12599296 | tf_op jit(solution)/shard_map/gather | solution.py:60
  40.1 6.6 %fusion = bf16[128,32,768]{2,1,0:T(8,128)(2,1)} fusion(bf16[128,32,768]{2,1,0:T(8,128)(2,1)} %bitcast.28, f32[128,32]{1,0:T(8,128)S(1)} %fusion.24), kind=kLoop, calls=%fused_computation.2 | loop fusion | flops 9437184 | bytes 12599296 | tf_op jit(solution)/shard_map/convert_element_type | solution.py:61
  46.6 0.0 all-to-all-done
  46.6 10.2 %all-to-all-start.1 = ((bf16[128,32,768]{2,1,0:T(8,128)(2,1)}), bf16[128,32,768]{2,1,0:T(8,128)(2,1)}, u32[]{:S(2)}, u32[]{:S(2)}) async-start(bf16[128,32,768]{2,1,0:T(8,128)(2,1)} %fusion), calls=%async_computation.1 | async-start | bytes 12582912 | tf_op jit(solution)/shard_map/all_to_all | solution.py:63
  56.8 0.0 all-gather.5.cloned.1.call-start
  56.8 0.0 copy-done
  56.9 1.7 multiply_reduce_fusion.1
  58.6 0.5 broadcast.58
  59.1 0.8 reduce.7
  59.9 0.1 eq.30
  60.0 74.0 %all-to-all-done.1 = bf16[128,32,768]{2,1,0:T(8,128)(2,1)} async-done(((bf16[128,32,768]{2,1,0:T(8,128)(2,1)}), bf16[128,32,768]{2,1,0:T(8,128)(2,1)}, u32[]{:S(2)}, u32[]{:S(2)}) %all-to-all-start.1) | async-done | bytes 6291488 | tf_op jit(solution)/shard_map/all_to_all | solution.py:63
  134.0 3.9 %multiply_reduce_fusion = (f32[128]{0:T(128)S(1)}, f32[128,768]{1,0:T(8,128)S(1)}) fusion(bf16[4096,768]{1,0:T(8,128)(2,1)} %bitcast.6, s32[4096]{0:T(1024)S(1)} %eq.30), kind=kOutput, calls=%fused_computation.30 | convolution fusion | flops 806027136 | bytes 6701568 | tf_op jit(solution)/shard_map/dot_general | solution.py:69
  137.9 0.1 multiply_convert_fusion
  138.0 0.8 pad_maximum_fusion
  138.8 0.0 all-gather.5.cloned.1.call-update
  138.8 0.0 all-gather.3.cloned.1.call-start
  138.9 0.7 all-gather.3.cloned.1.call-update
  139.6 0.2 reduce-scatter.3.cloned.1.call-start
  139.8 72.3 %all-gather.5.cloned.1.call-done = bf16[1024,1536]{1,0:T(8,128)(2,1)} async-done(((bf16[128,1536]{1,0:T(8,128)(2,1)}), bf16[1024,1536]{1,0:T(8,128)(2,1)}) %all-gather.5.cloned.1.call-update) | async-done | bytes 3145744 | tf_op jit(solution)/shard_map/all_gather | solution.py:17
  212.1 43.7 %all-gather.3.cloned.1.call-done = bf16[2048,1536]{1,0:T(8,128)(2,1)} async-done(((bf16[128,1536]{1,0:T(8,128)(2,1)}), bf16[2048,1536]{1,0:T(8,128)(2,1)}) %all-gather.3.cloned.1.call-update) | async-done | bytes 6291472 | tf_op jit(solution)/shard_map/all_gather | solution.py:17
  255.8 0.0 copy-start.2
  255.8 0.0 copy-start.3
  255.8 6.0 %fusion.5 = f32[2048,1024]{1,0:T(8,128)S(1)} fusion(bf16[2048,1536]{1,0:T(8,128)(2,1)} %all-gather.3.cloned.1.call-done, bf16[1024,1536]{1,0:T(8,128)(2,1)} %all-gather.5.cloned.1.call-done), kind=kOutput, calls=%fused_computation.8 | convolution fusion | flops 3221225472 | bytes 13107200 | tf_op jit(solution)/shard_map/dot_general | solution.py:83
  261.8 0.0 copy-done.2
  261.8 0.0 copy-done.3
  261.8 5.9 %fusion.8 = f32[2048,1024]{1,0:T(8,128)} fusion(bf16[2048,1536]{1,0:T(8,128)(2,1)S(1)} %copy-done.2, bf16[1024,1536]{1,0:T(8,128)(2,1)S(1)} %copy-done.3), kind=kOutput, calls=%fused_computation.11 | convolution fusion | flops 3221225472 | bytes 13107200 | tf_op jit(solution)/shard_map/dot_general | solution.py:80
  267.7 8.0 %fusion.11 = bf16[1024,768]{1,0:T(8,128)(2,1)S(1)} fusion(bf16[2048,1536]{1,0:T(8,128)(2,1)S(1)} %copy-done.2, f32[2048,1024]{1,0:T(8,128)} %fusion.8, f32[2048,1024]{1,0:T(8,128)S(1)} %fusion.5), kind=kOutput, calls=%fused_computation.16 | convolution fusion | flops 3230400512 | bytes 21495808 | tf_op jit(solution)/shard_map/dot_general | solution.py:88
  275.7 1.3 copy.12
  277.0 0.0 reduce-scatter.3.cloned.1.call-update
  277.0 0.0 reduce-scatter.5.cloned.1.call-start
  277.0 25.2 %reduce-scatter.3.cloned.1.call-done = bf16[2,128,768]{2,1,0:T(8,128)(2,1)} async-done(((bf16[8,128,768]{2,1,0:T(8,128)(2,1)}), bf16[2,128,768]{2,1,0:T(8,128)(2,1)}) %reduce-scatter.3.cloned.1.call-update) | async-done | bytes 393232 | tf_op jit(solution)/shard_map/reduce_scatter | solution.py:30
  302.2 0.0 reduce-scatter.5.cloned.1.call-update
  302.3 20.0 %reduce-scatter.5.cloned.1.call-done = bf16[1,128,768]{2,1,0:T(8,128)(2,1)} async-done(((bf16[2,128,768]{2,1,0:T(8,128)(2,1)}), bf16[1,128,768]{2,1,0:T(8,128)(2,1)}) %reduce-scatter.5.cloned.1.call-update) | async-done | bytes 196624 | tf_op jit(solution)/shard_map/reduce_scatter | solution.py:30
  322.3 1.1 fusion.17
  323.4 2.8 convolution_convert_fusion
  (3 shorter events, 0.0 us)
Async XLA Ops:
  6.5 50.3 %copy-start = (bf16[1920,768]{1,0:T(8,128)(2,1)S(1)}, bf16[1920,768]{1,0:T(8,128)(2,1)}, u32[]{:S(2)}) copy-start(bf16[1920,768]{1,0:T(8,128)(2,1)} %param.7) | copy-start | bytes 8847364
  6.5 15.6 %copy-start.1 = (bf16[80,768]{1,0:T(8,128)(2,1)S(1)}, bf16[80,768]{1,0:T(8,128)(2,1)}, u32[]{:S(2)}) copy-start(bf16[80,768]{1,0:T(8,128)(2,1)} %param.8) | copy-start | bytes 368644
  8.2 38.4 %all-to-all-start = ((s32[128,32,1]{1,2,0:T(1,128)}), s32[128,32,1]{1,2,0:T(1,128)S(1)}, u32[]{:S(2)}, u32[]{:S(2)}) async-start(s32[128,32,1]{1,2,0:T(1,128)} %bitcast), calls=%async_computation | async-start | bytes 131072 | tf_op jit(solution)/shard_map/all_to_all | solution.py:64
  46.6 87.3 %all-to-all-start.1 = ((bf16[128,32,768]{2,1,0:T(8,128)(2,1)}), bf16[128,32,768]{2,1,0:T(8,128)(2,1)}, u32[]{:S(2)}, u32[]{:S(2)}) async-start(bf16[128,32,768]{2,1,0:T(8,128)(2,1)} %fusion), calls=%async_computation.1 | async-start | bytes 12582912 | tf_op jit(solution)/shard_map/all_to_all | solution.py:63
  56.8 155.3 %all-gather.5.cloned.1.call-start = ((), (), s32[]{:S(2)}) async-start(), calls=%async_computation.5 | async-start | bytes 3538944 | tf_op jit(solution)/shard_map/all_gather | solution.py:17
  138.8 116.9 %all-gather.3.cloned.1.call-start = ((), (), s32[]{:S(2)}) async-start(), calls=%async_computation.4 | async-start | bytes 6684672 | tf_op jit(solution)/shard_map/all_gather | solution.py:17
  139.6 162.7 %reduce-scatter.3.cloned.1.call-start = ((), (), s32[]{:S(2)}) async-start(), calls=%async_computation.6 | async-start | bytes 1966080 | tf_op jit(solution)/shard_map/reduce_scatter | solution.py:30
  255.8 6.1 %copy-start.2 = (bf16[2048,1536]{1,0:T(8,128)(2,1)S(1)}, bf16[2048,1536]{1,0:T(8,128)(2,1)}, u32[]{:S(2)}) copy-start(bf16[2048,1536]{1,0:T(8,128)(2,1)} %all-gather.3.cloned.1.call-done) | copy-start | bytes 18874372
  255.8 6.1 %copy-start.3 = (bf16[1024,1536]{1,0:T(8,128)(2,1)S(1)}, bf16[1024,1536]{1,0:T(8,128)(2,1)}, u32[]{:S(2)}) copy-start(bf16[1024,1536]{1,0:T(8,128)(2,1)} %all-gather.5.cloned.1.call-done) | copy-start | bytes 9437188
  277.0 45.3 %reduce-scatter.5.cloned.1.call-start = ((), (), s32[]{:S(2)}) async-start(), calls=%async_computation.7 | async-start | bytes 589824 | tf_op jit(solution)/shard_map/reduce_scatter | solution.py:30
Sparse Core Ops, SparseCore 0:
  138.9 73.0 all-gather.4
  213.8 41.9 all-gather.2
  277.1 25.0 reduce-scatter.2
  304.4 17.8 reduce-scatter.4
where the time goes:
time: 333 us
  waiting for transfers between devices  236 us (71%)
  matrix products  28.3 us (8%)
  starting transfers between devices  22 us (7%)
  local copies, waits for them, and re-layouts  21.5 us (6%)
  between operations  13.3 us (4%)
  other arithmetic  11.8 us (4%)
    all_gather x2, waiting for transfers between devices, sent_together(): lax.all_gather(both, axis, axis=dim, tiled=True)  116 us
    all_to_all x1, waiting for transfers between devices, local(): lax.all_to_all(contrib, ROW_COL, split_axis=0, concat_axis=0, tiled=True)  74 us
    reduce_scatter x2, waiting for transfers between devices, own_block(): pieces = lax.psum_scatter(pieces, axes[k], scatter_dimension=0, tiled=True)  45.3 us
    gather x1, local copies, waits for them, and re-layouts, local(): rows = teacher[tube_index]  17.9 us
    all_to_all x1, starting transfers between devices, local(): lax.all_to_all(cell_index, ROW_COL, split_axis=0, concat_axis=0, tiled=True)  11.5 us
    all_to_all x1, starting transfers between devices, local(): lax.all_to_all(contrib, ROW_COL, split_axis=0, concat_axis=0, tiled=True)  10.2 us
    dot_general x1, matrix products, local(): lax.dot_general(slope, row_student, (((0,), (0,)), ((), ())), preferred_e...  7.98 us
  transfers between devices with their start and end apart: 6, of which 5 were waited for; matrix products, arithmetic and copies ran while one was open for 9% of the time, Pallas kernels for 0%

commit v1 on v0

v1 whole, which is shorter than its diff:
```python
import functools

import jax
import jax.numpy as jnp
from jax import lax
from jax.experimental import pallas as pl
from jax.experimental.pallas import tpu as pltpu
from jax.sharding import PartitionSpec as P

BOTH = ("row", "col")
MESH = pl.DeviceIdType.MESH
NT = (((1,), (1,)), ((), ()))

huber_delta = 0.05
norm_eps = 1e-06


class Place:
    def __init__(self):
        row, col = lax.axis_index("row"), lax.axis_index("col")
        self.zh, self.y = row // 4, row % 4
        self.x, self.zl, self.core = col // 4, (col // 2) % 2, col % 2

    def row_of(self, d, q):
        return (self.zh + q) % 2 * 4 + (self.y + d) % 4

    def a(self, d, q, k=0):
        col = (self.x + d) % 4 * 4 + (self.zl + q) % 2 * 2 + (self.core + k) % 2
        return (self.zh * 4 + self.y, col)

    def b(self, d, q):
        col = self.x * 4 + (self.zl + q) % 2 * 2 + self.core
        return (self.row_of(d, q), col)


def greet(peers):
    barrier = pltpu.get_barrier_semaphore()
    for peer in peers:
        pl.semaphore_signal(barrier, inc=1, device_id=peer, device_id_type=MESH)
    pl.semaphore_wait(barrier, len(peers))


def remote(src, dst, send, recv, i, device):
    return pltpu.make_async_remote_copy(
        src_ref=src,
        dst_ref=dst,
        send_sem=send.at[i],
        recv_sem=recv.at[i],
        device_id=device,
        device_id_type=MESH,
    )


def gather(own, buf, send, recv, to, cut, twin=None):
    rest = own.shape[0] - cut
    lo, hi = pl.ds(0, cut), pl.ds(cut, rest)
    ahead, behind, across = to(1, 0), to(3, 0), to(0, 1)
    plan = [
        (own, buf.at[3], ahead),
        (own, buf.at[1], behind),
        (own, buf.at[4], across),
        (buf.at[3, lo], buf.at[2, lo], ahead),
        (buf.at[1, hi], buf.at[2, hi], behind),
        (buf.at[4], buf.at[7], ahead),
        (buf.at[4], buf.at[5], behind),
        (buf.at[2, lo], buf.at[6, lo], across),
        (buf.at[2, hi], buf.at[6, hi], across),
    ]
    copies = [remote(s, d, send, recv, i, dev) for i, (s, d, dev) in enumerate(plan)]
    twins = []

    def pass_on(src, slot):
        if twin is not None:
            copy = remote(src, buf.at[8 + slot], send, recv, 9 + slot, twin)
            copy.start()
            twins.append(copy)

    for i in (0, 1, 2):
        copies[i].start()
    pass_on(own, 0)
    buf[0] = own[...]
    yield
    after = ((0, (3,), 3), (1, (4,), 1), (2, (5, 6), 4), (3, (7,), None), (4, (8,), 2))
    after += ((5, (), 7), (6, (), 5), (7, (), None), (8, (), 6))
    for i, starts, slot in after:
        copies[i].wait_recv()
        for j in starts:
            copies[j].start()
        if slot is not None:
            pass_on(buf.at[slot], slot)
        yield
    for copy in twins:
        copy.wait_recv()
    for copy in copies + twins:
        copy.wait_send()


def together(*plans):
    plans = list(plans)
    while plans:
        for plan in list(plans):
            try:
                next(plan)
            except StopIteration:
                plans.remove(plan)


def scatter(blocks, block_of, buf, send, recv, to):
    copies = []
    for q in (0, 1):
        for d in (1, 3, 2, 0):
            if q or d:
                slot = q * 4 + (4 - d) % 4
                src = blocks.at[block_of(d, q)]
                copies.append(remote(src, buf.at[slot], send, recv, slot, to(d, q)))
                copies[-1].start()
    buf[0] = blocks[block_of(0, 0)]
    yield
    for copy in copies:
        copy.wait_recv()
    for copy in copies:
        copy.wait_send()


def a_near(me):
    return [me.a(1, 0), me.a(3, 0), me.a(0, 1), me.a(0, 0, 1)]


def b_near(me):
    return [me.b(1, 0), me.b(3, 0), me.b(0, 1)]


def first_kernel(teacher, own, notes, teachers, column, told, s1, r1, s2, r2, s3, r3):
    me = Place()
    others = [(d, q, k) for k in (0, 1) for q in (0, 1) for d in range(4) if d or q or k]
    greet([me.a(*o) for o in others] + b_near(me))
    copies = []
    for d, q, k in others:
        twist = (me.zh + me.zl + q) % 2
        note = (me.x + d) % 4 * 4 + twist * 2 + (me.core + k) % 2
        slot = k * 8 + q * 4 + (4 - d) % 4
        copies.append(remote(notes.at[note], told.at[slot], s3, r3, slot, me.a(d, q, k)))
        copies[-1].start()
    told[0] = notes[me.x * 4 + (me.zh + me.zl) % 2 * 2 + me.core]
    together(
        gather(teacher, teachers, s1, r1, me.a, 48, me.a(0, 0, 1)),
        gather(own, column, s2, r2, me.b, 64),
    )
    for copy in copies:
        copy.wait_recv()
    for copy in copies:
        copy.wait_send()


def second_kernel(own, parts, line, arrived, s1, r1, s2, r2):
    me = Place()
    far = [me.b(d, q) for q in (0, 1) for d in range(4) if d or q]
    greet(a_near(me) + far)
    together(
        scatter(parts, me.row_of, arrived, s2, r2, me.b),
        gather(own, line, s1, r1, me.a, 64, me.a(0, 0, 1)),
    )


def third_kernel(own, line, column, s1, r1, s2, r2):
    me = Place()
    greet(a_near(me) + b_near(me))
    together(
        gather(own, line, s1, r1, me.a, 64, me.a(0, 0, 1)),
        gather(own, column, s2, r2, me.b, 64),
    )


def fourth_kernel(parts, arrived, s1, r1):
    me = Place()
    greet([me.b(d, q) for q in (0, 1) for d in range(4) if d or q])
    together(scatter(parts, lambda d, q: q * 4 + d, arrived, s1, r1, me.b))


def exchange(kernel, number, outs, sems, *args):
    return pl.pallas_call(
        kernel,
        out_shape=[jax.ShapeDtypeStruct(s, t) for s, t in outs],
        in_specs=[pl.BlockSpec(memory_space=pltpu.VMEM)] * len(args),
        out_specs=[pl.BlockSpec(memory_space=pltpu.VMEM)] * len(outs),
        scratch_shapes=[pltpu.SemaphoreType.DMA((n,)) for n in sems for _ in (0, 1)],
        compiler_params=pltpu.CompilerParams(
            collective_id=number, has_side_effects=True, vmem_limit_bytes=60 * 2**20
        ),
        name=kernel.__name__,
    )(*args)


def target_kernel(teachers, told, out, rows, picks):
    senders, tubes, _ = teachers.shape
    lane = lax.broadcasted_iota(jnp.int32, (1, 128), 1) // 32 * 128
    tube_at = lax.broadcasted_iota(jnp.int32, (tubes, 128), 0)
    cell_at = lax.broadcasted_iota(jnp.int32, (512, 128), 0)

    for half in (0, 1):

        @pl.loop(0, senders)
        def _(s):
            at = pl.ds(pl.multiple_of(s * 128, 128), 128)
            note = told[s]
            tube = note[half : half + 1].astype(jnp.int32)
            cell = note[2 + half : 3 + half].astype(jnp.int32) + lane
            scale = note[4 + half : 5 + half]
            select = jnp.where(tube_at == tube, 1.0, 0.0).astype(jnp.bfloat16)
            rows[at, :] = lax.dot_general(
                select, teachers[s], (((0,), (0,)), ((), ())), preferred_element_type=jnp.float32
            ).astype(jnp.bfloat16)
            picks[:, at] = jnp.where(cell_at == cell, scale, 0.0).astype(jnp.bfloat16)

        out[half * 512 : half * 512 + 512, :] = jnp.dot(
            picks[...], rows[...], preferred_element_type=jnp.float32
        ).astype(jnp.bfloat16)


def tile_kernel(line_s, line_t, column_s, column_t, out, slope):
    count = line_s.shape[0]

    @pl.loop(0, count // 256)
    def _(j):
        at = pl.ds(pl.multiple_of(j * 256, 256), 256)
        gram_s = lax.dot_general(column_s[...], line_s[at, :], NT, preferred_element_type=jnp.float32)
        gram_t = lax.dot_general(column_t[...], line_t[at, :], NT, preferred_element_type=jnp.float32)
        slope[:, at] = jnp.clip((gram_s - gram_t) / huber_delta, -1.0, 1.0).astype(jnp.bfloat16)

    @pl.loop(0, out.shape[0] // 256)
    def _(i):
        at = pl.ds(pl.multiple_of(i * 256, 256), 256)
        out[at, :] = jnp.dot(slope[at, :], line_s[...], preferred_element_type=jnp.float32).astype(
            jnp.bfloat16
        )


def plain(kernel, out, scratch, flops, *args):
    return pl.pallas_call(
        kernel,
        out_shape=jax.ShapeDtypeStruct(out, jnp.bfloat16),
        in_specs=[pl.BlockSpec(memory_space=pltpu.VMEM)] * len(args),
        out_specs=pl.BlockSpec(memory_space=pltpu.VMEM),
        scratch_shapes=[pltpu.VMEM(s, jnp.bfloat16) for s in scratch],
        compiler_params=pltpu.CompilerParams(vmem_limit_bytes=60 * 2**20),
        cost_estimate=pl.CostEstimate(flops=flops, bytes_accessed=2**23, transcendentals=0),
        name=kernel.__name__,
    )(*args)


def notes_of(block_map, block_counts, interp_weights):
    slots, peers = block_map.shape[2], block_counts.shape[1]
    per_peer = slots // peers
    levels = interp_weights.shape[0]
    fields = block_map[0]
    matches = fields[2][:, None] == jnp.arange(levels, dtype=jnp.int32)[None, :]
    weights = jnp.sum(jnp.where(matches, interp_weights[None, :], 0.0), axis=1)
    live = jnp.arange(per_peer, dtype=jnp.int32)[None, :] < block_counts[0][:, None]
    scale = weights * live.reshape(slots).astype(jnp.float32)
    notes = jnp.stack([fields[0].astype(jnp.float32), fields[1].astype(jnp.float32), scale])
    notes = notes.reshape(3, 2, 4, 4, 2, 2, per_peer)
    notes = jnp.stack([notes[:, 0], notes[:, 1, :, :, ::-1]], axis=1)
    notes = notes.transpose(3, 4, 5, 0, 1, 2, 6).reshape(16, 3 * 8 * per_peer // 128, 128)
    return jnp.pad(notes, ((0, 0), (0, 8 - notes.shape[1]), (0, 0)))


def local(student_hidden, projection, teacher, block_map, block_counts, interp_weights):
    tokens, width = student_hidden.shape[0], projection.shape[1]
    tubes = teacher.shape[0]
    bf16, f32 = jnp.bfloat16, jnp.float32
    notes = notes_of(block_map, block_counts, interp_weights)
    proj = jnp.dot(student_hidden, projection, preferred_element_type=f32)
    inverse = lax.rsqrt(jnp.sum(proj * proj, axis=1, keepdims=True) + norm_eps)
    unit = proj * inverse
    student_unit = unit.astype(bf16)

    block = (tokens, width)
    teachers, column_s, told = exchange(
        first_kernel,
        1,
        (((16, tubes, width), bf16), ((8, *block), bf16), ((16, 8, 128), f32)),
        (17, 9, 16),
        teacher,
        student_unit,
        notes,
    )
    parts = plain(
        target_kernel,
        (8 * tokens, width),
        ((2048, width), (512, 2048)),
        5 * 10**9,
        teachers,
        told,
    ).reshape(8, *block)
    line_s, arrived = exchange(
        second_kernel, 2, (((16, *block), bf16), ((8, *block), bf16)), (17, 8), student_unit, parts
    )
    target = jnp.sum(arrived.astype(f32), axis=0)
    teacher_unit = (
        target * lax.rsqrt(jnp.sum(target * target, axis=1, keepdims=True) + norm_eps)
    ).astype(bf16)
    line_t, column_t = exchange(
        third_kernel, 3, (((16, *block), bf16), ((8, *block), bf16)), (17, 9), teacher_unit
    )
    sums = plain(
        tile_kernel,
        (8 * tokens, width),
        ((8 * tokens, 16 * tokens),),
        10**10,
        line_s.reshape(-1, width),
        line_t.reshape(-1, width),
        column_s.reshape(-1, width),
        column_t.reshape(-1, width),
    ).reshape(8, *block)
    (summed,) = exchange(fourth_kernel, 4, (((8, *block), bf16),), (8,), sums)
    grad_unit = 2.0 * jnp.sum(summed.astype(f32), axis=0)
    along = jnp.sum(unit * grad_unit, axis=1, keepdims=True)
    grad_proj = ((grad_unit - unit * along) * inverse).astype(bf16)
    grad_hidden = lax.dot_general(grad_proj, projection, NT, preferred_element_type=f32)
    return grad_hidden.astype(bf16)


def solution(mesh):
    return jax.shard_map(
        local,
        mesh=mesh,
        in_specs=(
            P(BOTH, None),
            P(),
            P(BOTH, None),
            P(BOTH, None, None),
            P(BOTH, None),
            P(),
        ),
        out_specs=P(BOTH, None),
        check_vma=False,
    )
```

time: 333 us -> 168 us (0.50)
  waiting for transfers between devices: 236 us -> 0 us
  Pallas kernels: 0 us -> 152 us
  matrix products: 28.3 us -> 3.55 us
  starting transfers between devices: 22 us -> 0 us
  local copies, waits for them, and re-layouts: 21.5 us -> 2.61 us
  between operations: 13.3 us -> 0.14 us
    pallas_call x0 -> x6, Pallas kernels: none -> 152 us  [the longest x4 119 us: exchange(): pl.pallas_call(kernel, out_shape=[jax.ShapeDtypeStruct(s, t) for s, t in...]
    all_gather x2 -> x0, waiting for transfers between devices: 116 us -> none  [sent_together(): lax.all_gather(both, axis, axis=dim, tiled=True)]
    all_to_all x2 -> x0, waiting for transfers between devices: 74 us -> none  [the longest x1 74 us: local(): lax.all_to_all(contrib, ROW_COL, split_axis=0, concat_axis=0, tiled=True)]
    reduce_scatter x2 -> x0, waiting for transfers between devices: 45.3 us -> none  [own_block(): pieces = lax.psum_scatter(pieces, axes[k], scatter_dimension=0, tiled=True)]
    dot_general x6 -> x2, matrix products: 28.3 us -> 3.55 us  [the longest x1 1.86 us: local(): lax.dot_general(grad_proj, projection, NT, preferred_element_type=f32)]
    all_to_all x2 -> x0, starting transfers between devices: 21.6 us -> none  [the longest x1 11.5 us: local(): lax.all_to_all(cell_index, ROW_COL, split_axis=0, concat_axis=0, tiled=True)]
    gather x1 -> x0, local copies, waits for them, and re-layouts: 17.9 us -> none  [local(): rows = teacher[tube_index]]
    convert_element_type x1 -> x2, other arithmetic: 6.57 us -> 1.6 us  [the longest x1 0.82 us: notes_of(): fields[0].astype(jnp.float32)]
  transfers between devices with their start and end apart: 6 -> 0, of which waited for: 5 -> 0; matrix products, arithmetic and copies ran while one was open for 9% -> 0% of each run, Pallas kernels for 0% -> 0%
where the time goes in v1:
time: 168 us; the launch traced here: 167 us
  Pallas kernels  152 us (90%)
  other arithmetic  8.83 us (5%)
  matrix products  3.55 us (2%)
  local copies, waits for them, and re-layouts  2.61 us (2%)
    pallas_call x4, Pallas kernels, exchange(): pl.pallas_call(kernel, out_shape=[jax.ShapeDtypeStruct(s, t) for s, t in...  119 us
    pallas_call x2, Pallas kernels, plain(): pl.pallas_call(kernel, out_shape=jax.ShapeDtypeStruct(out, jnp.bfloat16),...  33.3 us

profile of v1, /device:TPU:1, one launch (start us, length us, event | category | flops | bytes accessed | tf_op | source)
XLA Modules:
  0.0 167.3 jit_solution(6015846901895291737)
XLA Ops:
  0.0 0.0 copy-start
  0.0 0.5 broadcast.55
  0.5 1.6 reduce.11
  2.1 0.7 slice.20
  2.8 0.9 select_reduce_fusion
  3.7 0.2 lt.25
  3.9 0.8 convert_reduce_fusion.3
  4.7 0.1 convert_element_type.51
  4.8 0.1 reduce_sum.58
  4.9 0.1 compare_select_fusion
  5.1 0.1 convert_element_type.53
  5.2 0.1 pad_maximum_fusion
  5.4 0.1 maximum_bitcast_fusion
  5.5 0.1 copy.14
  5.6 0.1 reshape.109
  5.7 0.6 pad.4.notes
  6.3 0.0 copy-done
  6.3 1.7 %multiply_reduce_fusion.2 = (f32[128]{0:T(128)S(1)}, f32[128,768]{1,0:T(8,128)S(1)}) fusion(bf16[128,1920]{1,0:T(8,128)(2,1)} %param.6, bf16[1920,768]{1,0:T(8,128)(2,1)S(1)} %copy-done), kind=kOutput, calls=%fused_computation.9 | convolution fusion | flops 377683840 | bytes 3834368 | tf_op jit(solution)/shard_map/dot_general | solution.py:272
  8.0 0.8 multiply_convert_fusion.2.own
  8.8 28.2 %first_kernel.1 = (bf16[16,80,768]{2,1,0:T(8,128)(2,1)}, bf16[8,128,768]{2,1,0:T(8,128)(2,1)}, f32[16,8,128]{2,1,0:T(8,128)}) custom-call(bf16[80,768]{1,0:T(8,128)(2,1)} %teacher.1, bf16[128,768]{1,0:T(8,128)(2,1)} %multiply_convert_fusion.2.own, f32[16,8,128]{2,1,0:T(8,128)} %pad.4.notes), custom_call_target="tpu_custom_call" | custom-call | tf_op jit(solution)/shard_map/first_kernel/pallas_call | solution.py:181
  37.1 16.2 %target_kernel.1 = bf16[1024,768]{1,0:T(8,128)(2,1)} custom-call(bf16[16,80,768]{2,1,0:T(8,128)(2,1)} %get-tuple-element.12.teachers, f32[16,8,128]{2,1,0:T(8,128)} %get-tuple-element.13.told), custom_call_target="tpu_custom_call" | custom-call | flops 5000000000 | bytes 8388608 | tf_op jit(solution)/shard_map/target_kernel/pallas_call | solution.py:239
  53.3 39.8 %second_kernel.1 = (bf16[16,128,768]{2,1,0:T(8,128)(2,1)}, bf16[8,128,768]{2,1,0:T(8,128)(2,1)}) custom-call(bf16[128,768]{1,0:T(8,128)(2,1)} %multiply_convert_fusion.2.own, bf16[8,128,768]{2,1,0:T(8,128)(2,1)} %bitcast.12), custom_call_target="tpu_custom_call" | custom-call | tf_op jit(solution)/shard_map/second_kernel/pallas_call | solution.py:181
  93.2 1.7 convert_reduce_fusion.1
  94.8 0.1 multiply_reduce_fusion.1
  95.0 0.8 multiply_convert_fusion.1.own
  95.7 22.6 %third_kernel.1 = (bf16[16,128,768]{2,1,0:T(8,128)(2,1)}, bf16[8,128,768]{2,1,0:T(8,128)(2,1)}) custom-call(bf16[128,768]{1,0:T(8,128)(2,1)} %multiply_convert_fusion.1.own), custom_call_target="tpu_custom_call" | custom-call | tf_op jit(solution)/shard_map/third_kernel/pallas_call | solution.py:181
  118.3 17.0 %tile_kernel.1 = bf16[1024,768]{1,0:T(8,128)(2,1)} custom-call(bf16[2048,768]{1,0:T(8,128)(2,1)} %bitcast.15, bf16[2048,768]{1,0:T(8,128)(2,1)} %bitcast.16, bf16[1024,768]{1,0:T(8,128)(2,1)} %bitcast.17, bf16[1024,768]{1,0:T(8,128)(2,1)} %bitcast.18), custom_call_target="tpu_custom_call" | custom-call | flops 10000000000 | bytes 8388608 | tf_op jit(solution)/shard_map/tile_kernel/pallas_call | solution.py:239
  135.3 28.3 %fourth_kernel.1 = bf16[8,128,768]{2,1,0:T(8,128)(2,1)} custom-call(bf16[8,128,768]{2,1,0:T(8,128)(2,1)} %bitcast.13), custom_call_target="tpu_custom_call" | custom-call | tf_op jit(solution)/shard_map/fourth_kernel/pallas_call | solution.py:181
  163.6 1.7 convert_reduce_fusion
  165.3 0.2 multiply_reduce_fusion
  165.5 1.9 %convolution_convert_fusion = bf16[128,1920]{1,0:T(8,128)(2,1)} fusion(bf16[1920,768]{1,0:T(8,128)(2,1)S(1)} %copy-done, f32[128,768]{1,0:T(8,128)S(1)} %convert_reduce_fusion, f32[128,768]{1,0:T(8,128)S(1)} %get-tuple-element.24, f32[128]{0:T(128)S(1)} %multiply_reduce_fusion, f32[128]{0:T(128)S(1)} %add_rsqrt_fusion.1), kind=kOutput, calls=%fused_computation.2 | convolution fusion | flops 378322944 | bytes 4228096 | tf_op jit(solution)/shard_map/dot_general | solution.py:319
  (4 shorter events, 0.1 us)
Async XLA Ops:
  0.0 6.3 %copy-start = (bf16[1920,768]{1,0:T(8,128)(2,1)S(1)}, bf16[1920,768]{1,0:T(8,128)(2,1)}, u32[]{:S(2)}) copy-start(bf16[1920,768]{1,0:T(8,128)(2,1)} %param.7) | copy-start | bytes 8847364

commit v2 on v1

v2 whole, which is shorter than its diff:
```python
import jax
import jax.numpy as jnp
from jax import lax
from jax.experimental import pallas as pl
from jax.experimental.pallas import tpu as pltpu
from jax.sharding import PartitionSpec as P

BOTH = ("row", "col")
MESH = pl.DeviceIdType.MESH
NT = (((1,), (1,)), ((), ()))

huber_delta = 0.05
norm_eps = 1e-06


class Place:
    def __init__(self):
        row, col = lax.axis_index("row"), lax.axis_index("col")
        self.zh, self.y = row // 4, row % 4
        self.x, self.zl, self.core = col // 4, (col // 2) % 2, col % 2

    def row_of(self, d, q):
        return (self.zh + q) % 2 * 4 + (self.y + d) % 4

    def a(self, d, q, k=0):
        col = (self.x + d) % 4 * 4 + (self.zl + q) % 2 * 2 + (self.core + k) % 2
        return (self.zh * 4 + self.y, col)

    def b(self, d, q):
        col = self.x * 4 + (self.zl + q) % 2 * 2 + self.core
        return (self.row_of(d, q), col)


def greet(peers):
    barrier = pltpu.get_barrier_semaphore()
    for peer in peers:
        pl.semaphore_signal(barrier, inc=1, device_id=peer, device_id_type=MESH)
    pl.semaphore_wait(barrier, len(peers))


def remote(src, dst, send, recv, i, device):
    return pltpu.make_async_remote_copy(
        src_ref=src,
        dst_ref=dst,
        send_sem=send.at[i],
        recv_sem=recv.at[i],
        device_id=device,
        device_id_type=MESH,
    )


def rows_of(ref, at, count):
    return ref.at[pl.ds(pl.multiple_of(at, 16), count)]


def gather(own, buf, sems, to, cut, ends, twin=None):
    send, recv = sems
    n = own.shape[0]

    def part(block, start=0, count=n):
        return rows_of(buf, block * n + start, count)

    ahead, behind, across = to(1, 0), to(3, 0), to(0, 1)
    lo, hi = (0, cut), (cut, n - cut)
    plan = [
        (own, part(3), ahead),
        (own, part(1), behind),
        (own, part(4), across),
        (part(3, *lo), part(2, *lo), ahead),
        (part(1, *hi), part(2, *hi), behind),
        (part(4), part(7), ahead),
        (part(4), part(5), behind),
        (part(2, *lo), part(6, *lo), across),
        (part(2, *hi), part(6, *hi), across),
    ]
    copies = [remote(s, d, send, recv, i, dev) for i, (s, d, dev) in enumerate(plan)]
    ends.extend(copies)
    twins = []

    def pass_on(src, block):
        if twin is not None:
            copy = remote(src, part(8 + block), send, recv, 9 + block, twin)
            copy.start()
            twins.append(copy)
            ends.append(copy)

    for i in (0, 1, 2):
        copies[i].start()
    pass_on(own, 0)
    buf[0:n, :] = own[...]
    yield
    after = ((0, (3,), 3), (1, (4,), 1), (2, (5, 6), 4), (3, (7,), None), (4, (8,), 2))
    after += ((5, (), 7), (6, (), 5), (7, (), None), (8, (), 6))
    for i, starts, block in after:
        copies[i].wait_recv()
        for j in starts:
            copies[j].start()
        if block is not None:
            pass_on(part(block), block)
        yield
    for copy in twins:
        copy.wait_recv()


def reduce(blocks, block_of, land, sums, sems, to, ends, total):
    send, recv = sems
    n = total.shape[0]
    half = n // 2
    ahead, behind, across = to(1, 0), to(3, 0), to(0, 1)

    def mine(d, q, start=0, count=n):
        return rows_of(blocks, block_of(d, q) * n + start, count)

    def at(ref, slot, start=0, count=n):
        return rows_of(ref, slot * n + start, count)

    def wide(ref):
        return ref[...].astype(jnp.float32)

    lo, hi = (0, half), (half, half)
    plan = [
        (mine(2, 1), at(land, 0), across),
        (mine(1, 1), at(land, 1), ahead),
        (mine(3, 1), at(land, 2), behind),
        (at(sums, 0, *lo), at(land, 3, *lo), ahead),
        (at(sums, 0, *hi), at(land, 3, *hi), behind),
        (at(sums, 1), at(land, 4), across),
        (mine(1, 0, *hi), at(land, 5, *hi), ahead),
        (at(sums, 2, *lo), at(land, 5, *lo), ahead),
        (mine(3, 0, *lo), at(land, 6, *lo), behind),
        (at(sums, 2, *hi), at(land, 6, *hi), behind),
    ]
    copies = [remote(s, d, send, recv, i, dev) for i, (s, d, dev) in enumerate(plan)]
    ends.extend(copies)

    def store(slot, start, count, *terms):
        value = wide(terms[0])
        for term in terms[1:]:
            value = value + wide(term)
        at(sums, slot, start, count)[...] = value.astype(jnp.bfloat16)

    copies[0].start()
    copies[2].start()
    copies[1].start()
    yield
    copies[6].start()
    copies[8].start()
    yield
    copies[0].wait_recv()
    store(0, 0, n, mine(2, 0), at(land, 0))
    copies[3].start()
    copies[4].start()
    yield
    copies[1].wait_recv()
    copies[2].wait_recv()
    store(1, 0, n, mine(0, 1), at(land, 1), at(land, 2))
    copies[5].start()
    yield
    copies[3].wait_recv()
    store(2, *lo, mine(1, 0, *lo), at(land, 3, *lo))
    copies[7].start()
    copies[4].wait_recv()
    store(2, *hi, mine(3, 0, *hi), at(land, 3, *hi))
    copies[9].start()
    yield
    for i in (6, 8, 5, 7, 9):
        copies[i].wait_recv()
    total[...] = wide(mine(0, 0)) + wide(at(land, 4)) + wide(at(land, 5)) + wide(at(land, 6))


def step(*plans):
    for plan in plans:
        next(plan, None)


def finish(*plans):
    plans = list(plans)
    while plans:
        for plan in list(plans):
            try:
                next(plan)
            except StopIteration:
                plans.remove(plan)


def whole_kernel(
    teacher, own_s, notes, total,
    teachers, told, rows, picks, parts, line_s, column_s, line_t, column_t, own_t, gram, slope,
    land_0, sums_0, land_1, sums_1, *sems,
):
    f32, bf16 = jnp.float32, jnp.bfloat16
    pairs = [sems[i : i + 2] for i in range(0, len(sems), 2)]
    me = Place()
    twin = me.a(0, 0, 1)
    tubes, tokens = teacher.shape[0], own_s.shape[0]
    others = [(d, q, k) for k in (0, 1) for q in (0, 1) for d in range(4) if d or q or k]
    greet([me.a(*o) for o in others] + [me.b(1, 0), me.b(3, 0), me.b(0, 1)])
    ends = []

    teach = gather(teacher, teachers, pairs[0], me.a, 48, ends, twin)
    step(teach)
    told_by = []
    for d, q, k in others:
        twist = (me.zh + me.zl + q) % 2
        note = (me.x + d) % 4 * 4 + twist * 2 + (me.core + k) % 2
        slot = k * 8 + q * 4 + (4 - d) % 4
        copy = remote(notes.at[note], told.at[slot], *pairs[1], slot, me.a(d, q, k))
        copy.start()
        told_by.append(copy)
        ends.append(copy)
    told[0] = notes[me.x * 4 + (me.zh + me.zl) % 2 * 2 + me.core]
    spread = gather(own_s, column_s, pairs[2], me.b, 64, ends)
    step(spread)
    for _ in range(5):
        step(teach, spread)
    align = gather(own_s, line_s, pairs[3], me.a, 64, ends, twin)
    step(align)
    for copy in told_by:
        copy.wait_recv()
    finish(teach, spread)

    lane = lax.broadcasted_iota(jnp.int32, (1, 128), 1) // 32 * 128
    tube_at = lax.broadcasted_iota(jnp.int32, (tubes, 128), 0)
    cell_at = lax.broadcasted_iota(jnp.int32, (4 * tokens, 128), 0)

    def weigh(first, last):
        @pl.loop(first, last)
        def _(s):
            at = pl.ds(pl.multiple_of(s * 128, 128), 128)
            note = told[s]
            features = teachers[pl.ds(pl.multiple_of(s * tubes, 16), tubes), :]
            for half in (0, 1):
                tube = note[half : half + 1].astype(jnp.int32)
                cell = note[2 + half : 3 + half].astype(jnp.int32) + lane
                scale = note[4 + half : 5 + half]
                select = jnp.where(tube_at == tube, 1.0, 0.0).astype(bf16)
                rows[half, at, :] = lax.dot_general(
                    select, features, (((0,), (0,)), ((), ())), preferred_element_type=f32
                ).astype(bf16)
                picks[half, :, at] = jnp.where(cell_at == cell, scale, 0.0).astype(bf16)

    def add_up(half):
        at = pl.ds(pl.multiple_of(half * 4 * tokens, 128), 4 * tokens)
        parts[at, :] = jnp.dot(picks[half], rows[half], preferred_element_type=f32).astype(bf16)

    weigh(0, 8)
    step(align)
    weigh(8, 16)
    step(align)
    merge = reduce(parts, me.row_of, land_0, sums_0, pairs[4], me.b, ends, total)
    add_up((me.zh + 1) % 2)
    step(merge, align)
    add_up(me.zh)
    finish(merge, align)
    target = total[...]
    own_t[...] = (
        target * lax.rsqrt(jnp.sum(target * target, axis=1, keepdims=True) + norm_eps)
    ).astype(bf16)

    line = gather(own_t, line_t, pairs[5], me.a, 64, ends, twin)
    column = gather(own_t, column_t, pairs[6], me.b, 64, ends)
    step(line, column)
    wide = 256

    def student(first, last):
        @pl.loop(first, last)
        def _(j):
            at = pl.ds(pl.multiple_of(j * wide, wide), wide)
            gram[:, at] = lax.dot_general(
                column_s[...], line_s[at, :], NT, preferred_element_type=f32
            )

    student(0, 4)
    for j in range(4, 8):
        step(line, column)
        student(j, j + 1)
    finish(line, column)

    @pl.loop(0, 16 * tokens // wide)
    def _(j):
        at = pl.ds(pl.multiple_of(j * wide, wide), wide)
        gram_t = lax.dot_general(column_t[...], line_t[at, :], NT, preferred_element_type=f32)
        slope[:, at] = jnp.clip((gram[:, at] - gram_t) * (1.0 / huber_delta), -1.0, 1.0).astype(bf16)

    def pull(first, last):
        @pl.loop(first, last)
        def _(i):
            at = pl.ds(pl.multiple_of(i * wide, wide), wide)
            parts[at, :] = jnp.dot(slope[at, :], line_s[...], preferred_element_type=f32).astype(bf16)

    for copy in ends:
        copy.wait_send()
    ends.clear()
    merge = reduce(
        parts, lambda d, q: q * 4 + d, land_1, sums_1, pairs[7], me.b, ends, total
    )
    pull(2, 4)
    step(merge)
    pull(0, 2)
    finish(merge)
    for copy in ends:
        copy.wait_send()


def whole(teacher, own, notes):
    tubes, (tokens, width) = teacher.shape[0], own.shape
    f32, bf16 = jnp.float32, jnp.bfloat16
    buffers = (
        ((16 * tubes, width), bf16),
        ((16, 8, 128), f32),
        ((2, 2048, width), bf16),
        ((2, 4 * tokens, 2048), bf16),
        ((8 * tokens, width), bf16),
        ((16 * tokens, width), bf16),
        ((8 * tokens, width), bf16),
        ((16 * tokens, width), bf16),
        ((8 * tokens, width), bf16),
        ((tokens, width), bf16),
        ((8 * tokens, 16 * tokens), f32),
        ((8 * tokens, 16 * tokens), bf16),
        ((7 * tokens, width), bf16),
        ((3 * tokens, width), bf16),
        ((7 * tokens, width), bf16),
        ((3 * tokens, width), bf16),
    )
    sems = (17, 16, 9, 17, 10, 17, 9, 10)
    return pl.pallas_call(
        whole_kernel,
        out_shape=jax.ShapeDtypeStruct((tokens, width), f32),
        in_specs=[pl.BlockSpec(memory_space=pltpu.VMEM)] * 3,
        out_specs=pl.BlockSpec(memory_space=pltpu.VMEM),
        scratch_shapes=[pltpu.VMEM(*b) for b in buffers]
        + [pltpu.SemaphoreType.DMA((n,)) for n in sems for _ in (0, 1)],
        compiler_params=pltpu.CompilerParams(
            collective_id=1, has_side_effects=True, vmem_limit_bytes=60 * 2**20
        ),
        name="whole_kernel",
    )(teacher, own, notes)


def notes_of(block_map, block_counts, interp_weights):
    slots, peers = block_map.shape[2], block_counts.shape[1]
    per_peer = slots // peers
    levels = interp_weights.shape[0]
    fields = block_map[0]
    matches = fields[2][:, None] == jnp.arange(levels, dtype=jnp.int32)[None, :]
    weights = jnp.sum(jnp.where(matches, interp_weights[None, :], 0.0), axis=1)
    live = jnp.arange(per_peer, dtype=jnp.int32)[None, :] < block_counts[0][:, None]
    scale = weights * live.reshape(slots).astype(jnp.float32)
    notes = jnp.stack([fields[0].astype(jnp.float32), fields[1].astype(jnp.float32), scale])
    notes = notes.reshape(3, 2, 4, 4, 2, 2, per_peer)
    notes = jnp.stack([notes[:, 0], notes[:, 1, :, :, ::-1]], axis=1)
    notes = notes.transpose(3, 4, 5, 0, 1, 2, 6).reshape(16, 3 * 8 * per_peer // 128, 128)
    return jnp.pad(notes, ((0, 0), (0, 8 - notes.shape[1]), (0, 0)))


def local(student_hidden, projection, teacher, block_map, block_counts, interp_weights):
    bf16, f32 = jnp.bfloat16, jnp.float32
    notes = notes_of(block_map, block_counts, interp_weights)
    proj = jnp.dot(student_hidden, projection, preferred_element_type=f32)
    inverse = lax.rsqrt(jnp.sum(proj * proj, axis=1, keepdims=True) + norm_eps)
    unit = proj * inverse
    student_unit = unit.astype(bf16)

    grad_unit = 2.0 * whole(teacher, student_unit, notes)
    along = jnp.sum(unit * grad_unit, axis=1, keepdims=True)
    grad_proj = ((grad_unit - unit * along) * inverse).astype(bf16)
    grad_hidden = lax.dot_general(grad_proj, projection, NT, preferred_element_type=f32)
    return grad_hidden.astype(bf16)


def solution(mesh):
    return jax.shard_map(
        local,
        mesh=mesh,
        in_specs=(
            P(BOTH, None),
            P(),
            P(BOTH, None),
            P(BOTH, None, None),
            P(BOTH, None),
            P(),
        ),
        out_specs=P(BOTH, None),
        check_vma=False,
    )
```

time: 168 us -> 106 us (0.63)
  Pallas kernels: 152 us -> 91.7 us
  other arithmetic: 8.83 us -> 5.61 us
    pallas_call x6 -> x1, Pallas kernels: 152 us -> 91.7 us  [whole(): pl.pallas_call(whole_kernel, out_shape=jax.ShapeDtypeStruct((tokens, widt...]
    reduce_sum x3 -> x0, other arithmetic: 3.43 us -> none  [the longest x1 1.66 us: local(): target = jnp.sum(arrived.astype(f32), axis=0)]
where the time goes in v2:
time: 106 us; the launch traced here: 105 us
  Pallas kernels  91.7 us (87%)
  other arithmetic  5.61 us (5%)
  matrix products  4.52 us (4%)
  local copies, waits for them, and re-layouts  2.61 us (2%)
    pallas_call x1, Pallas kernels, whole(): pl.pallas_call(whole_kernel, out_shape=jax.ShapeDtypeStruct((tokens, widt...  91.7 us
    dot_general x1, matrix products, local(): lax.dot_general(grad_proj, projection, NT, preferred_element_type=f32)  2.83 us

profile of v2, /device:TPU:1, one launch (start us, length us, event | category | flops | bytes accessed | tf_op | source)
XLA Modules:
  0.0 104.5 jit_solution(13306950602410829041)
XLA Ops:
  0.0 0.0 copy-start
  0.0 0.5 broadcast.44
  0.5 1.6 %reduce.11 = s32[128]{0:T(128)S(1)} reduce(s32[1,128]{1,0:T(1,128)} %param.10, s32[]{:T(128)} %broadcast.44), dimensions={0}, to_apply=%param.10.reduce_sub_computation.3 | reduce | bytes 1028 | tf_op args[4]
  2.1 0.7 slice.20
  2.8 0.9 select_reduce_fusion
  3.7 0.2 lt.25
  3.9 0.8 convert_reduce_fusion.1
  4.7 0.1 convert_element_type.42
  4.8 0.1 reduce_sum.31
  4.9 0.1 compare_select_fusion
  5.1 0.1 convert_element_type.44
  5.2 0.1 pad_maximum_fusion
  5.4 0.1 maximum_bitcast_fusion
  5.5 0.1 copy.14
  5.6 0.1 reshape.79
  5.7 0.6 pad.4.notes
  6.3 0.0 copy-done
  6.3 1.7 %multiply_reduce_fusion.1 = (f32[128]{0:T(128)S(1)}, f32[128,768]{1,0:T(8,128)S(1)}) fusion(bf16[128,1920]{1,0:T(8,128)(2,1)} %param.6, bf16[1920,768]{1,0:T(8,128)(2,1)S(1)} %copy-done), kind=kOutput, calls=%fused_computation.5 | convolution fusion | flops 377683840 | bytes 3834368 | tf_op jit(solution)/shard_map/dot_general | solution.py:360
  8.0 0.8 multiply_convert_fusion.1.own_s
  8.8 91.7 %whole_kernel.1 = f32[128,768]{1,0:T(8,128)} custom-call(bf16[80,768]{1,0:T(8,128)(2,1)} %teacher.1, bf16[128,768]{1,0:T(8,128)(2,1)} %multiply_convert_fusion.1.own_s, f32[16,8,128]{2,1,0:T(8,128)} %pad.4.notes), custom_call_target="tpu_custom_call" | custom-call | tf_op jit(solution)/shard_map/whole_kernel/pallas_call | solution.py:327
  100.5 1.2 %multiply_reduce_fusion = f32[128]{0:T(128)S(1)} fusion(f32[128,768]{1,0:T(8,128)} %whole_kernel.1, f32[128,768]{1,0:T(8,128)S(1)} %get-tuple-element.10, f32[128]{0:T(128)S(1)} %add_rsqrt_fusion), kind=kLoop, calls=%fused_computation.4 | loop fusion | flops 393088 | bytes 787456 | tf_op jit(solution)/shard_map/reduce_sum | solution.py:366
  101.7 2.8 %convolution_convert_fusion = bf16[128,1920]{1,0:T(8,128)(2,1)} fusion(bf16[1920,768]{1,0:T(8,128)(2,1)S(1)} %copy-done, f32[128,768]{1,0:T(8,128)} %whole_kernel.1, f32[128,768]{1,0:T(8,128)S(1)} %get-tuple-element.10, f32[128]{0:T(128)S(1)} %multiply_reduce_fusion, f32[128]{0:T(128)S(1)} %add_rsqrt_fusion), kind=kOutput, calls=%fused_computation | convolution fusion | flops 378322944 | bytes 4228096 | tf_op jit(solution)/shard_map/dot_general | solution.py:368
  (3 shorter events, 0.1 us)
Async XLA Ops:
  0.0 6.3 %copy-start = (bf16[1920,768]{1,0:T(8,128)(2,1)S(1)}, bf16[1920,768]{1,0:T(8,128)(2,1)}, u32[]{:S(2)}) copy-start(bf16[1920,768]{1,0:T(8,128)(2,1)} %param.7) | copy-start | bytes 8847364

commit v3 on v2

--- a/solution.py
+++ b/solution.py
@@ -53,12 +53,14 @@
     return ref.at[pl.ds(pl.multiple_of(at, 16), count)]
 
 
-def gather(own, buf, sems, to, cut, ends, twin=None):
+def gather(own, buf, sems, to, cut, ends, twin=None, off=0, n=None):
     send, recv = sems
-    n = own.shape[0]
+    size = own.shape[0]
+    n = n or size
+    own = rows_of(own, off, n)
 
     def part(block, start=0, count=n):
-        return rows_of(buf, block * n + start, count)
+        return rows_of(buf, block * size + off + start, count)
 
     ahead, behind, across = to(1, 0), to(3, 0), to(0, 1)
     lo, hi = (0, cut), (cut, n - cut)
@@ -87,7 +89,7 @@
     for i in (0, 1, 2):
         copies[i].start()
     pass_on(own, 0)
-    buf[0:n, :] = own[...]
+    buf[off : off + n, :] = own[...]
     yield
     after = ((0, (3,), 3), (1, (4,), 1), (2, (5, 6), 4), (3, (7,), None), (4, (8,), 2))
     after += ((5, (), 7), (6, (), 5), (7, (), None), (8, (), 6))
@@ -102,17 +104,18 @@
         copy.wait_recv()
 
 
-def reduce(blocks, block_of, land, sums, sems, to, ends, total):
+def reduce(blocks, block_of, land, sums, sems, to, ends, total, off=0, n=None):
     send, recv = sems
-    n = total.shape[0]
+    size = total.shape[0]
+    n = n or size
     half = n // 2
     ahead, behind, across = to(1, 0), to(3, 0), to(0, 1)
 
     def mine(d, q, start=0, count=n):
-        return rows_of(blocks, block_of(d, q) * n + start, count)
+        return rows_of(blocks, block_of(d, q) * size + off + start, count)
 
     def at(ref, slot, start=0, count=n):
-        return rows_of(ref, slot * n + start, count)
+        return rows_of(ref, slot * size + off + start, count)
 
     def wide(ref):
         return ref[...].astype(jnp.float32)
@@ -141,6 +144,7 @@
 
     copies[0].start()
     copies[2].start()
+    yield
     copies[1].start()
     yield
     copies[6].start()
@@ -165,12 +169,18 @@
     yield
     for i in (6, 8, 5, 7, 9):
         copies[i].wait_recv()
-    total[...] = wide(mine(0, 0)) + wide(at(land, 4)) + wide(at(land, 5)) + wide(at(land, 6))
+    landed = wide(at(land, 4)) + wide(at(land, 5)) + wide(at(land, 6))
+    total[off : off + n, :] = wide(mine(0, 0)) + landed
 
 
 def step(*plans):
     for plan in plans:
         next(plan, None)
+
+
+def steps(count, *plans):
+    for _ in range(count):
+        step(*plans)
 
 
 def finish(*plans):
@@ -183,22 +193,62 @@
                 plans.remove(plan)
 
 
+def write_notes(block_map, block_counts, interp_weights, before, notes):
+    f32, i32 = jnp.float32, jnp.int32
+    for y in range(4):
+        for x in range(4):
+            for zh in (0, 1):
+                chunk = (zh * 4 + y) * 4 + x
+                row = y * 8 + x * 2 + zh
+                for field in range(3):
+                    before[field, row : row + 1, :] = block_map[field, chunk : chunk + 1, :]
+    row = lax.broadcasted_iota(i32, (32, 128), 0)
+    column = lax.broadcasted_iota(i32, (32, 128), 1)
+    chunk = (row % 2 * 4 + row // 8) * 4 + row % 8 // 2
+    counts = jnp.where(column // 4 == chunk, block_counts[...], 0).astype(f32).astype(jnp.bfloat16)
+    source = lax.broadcasted_iota(i32, (128, 128), 0)
+    lane = lax.broadcasted_iota(i32, (128, 128), 1)
+    spread = jnp.where(source % 4 == lane // 32, 1.0, 0.0).astype(jnp.bfloat16)
+    counts = jnp.dot(counts, spread, preferred_element_type=f32).astype(i32)
+    level = before[2]
+    scale = jnp.zeros((32, 128), f32)
+    for l in range(interp_weights.shape[0]):
+        scale = jnp.where(level == l, interp_weights[l], scale)
+    scale = jnp.where(column % 32 < counts, scale, 0.0)
+    notes[...] = jnp.zeros_like(notes)
+    for field, value in enumerate((before[0].astype(f32), before[1].astype(f32), scale)):
+        for g in range(4):
+            pieces = [value[y * 8 : y * 8 + 8, g * 32 : g * 32 + 32] for y in range(4)]
+            turned = jnp.concatenate(pieces, axis=1)
+            for x in range(4):
+                for zh in (0, 1):
+                    note = x * 4 + (g // 2 + zh) % 2 * 2 + g % 2
+                    at = field * 2 + zh
+                    notes[note, at : at + 1, :] = turned[x * 2 + zh : x * 2 + zh + 1]
+
+
 def whole_kernel(
-    teacher, own_s, notes, total,
+    hidden_in, projection_in, teacher, block_map, block_counts, interp_weights, out,
+    hidden, projection, before, notes, unit, total, own_s,
     teachers, told, rows, picks, parts, line_s, column_s, line_t, column_t, own_t, gram, slope,
-    land_0, sums_0, land_1, sums_1, *sems,
+    land_0, sums_0, land_1, sums_1, loads, *sems,
 ):
     f32, bf16 = jnp.float32, jnp.bfloat16
     pairs = [sems[i : i + 2] for i in range(0, len(sems), 2)]
     me = Place()
     twin = me.a(0, 0, 1)
     tubes, tokens = teacher.shape[0], own_s.shape[0]
+    load_hidden = pltpu.make_async_copy(hidden_in, hidden, loads.at[0])
+    load_projection = pltpu.make_async_copy(projection_in, projection, loads.at[1])
+    load_hidden.start()
+    load_projection.start()
     others = [(d, q, k) for k in (0, 1) for q in (0, 1) for d in range(4) if d or q or k]
     greet([me.a(*o) for o in others] + [me.b(1, 0), me.b(3, 0), me.b(0, 1)])
     ends = []
 
     teach = gather(teacher, teachers, pairs[0], me.a, 48, ends, twin)
     step(teach)
+    write_notes(block_map, block_counts, interp_weights, before, notes)
     told_by = []
     for d, q, k in others:
         twist = (me.zh + me.zl + q) % 2
@@ -209,15 +259,19 @@
         told_by.append(copy)
         ends.append(copy)
     told[0] = notes[me.x * 4 + (me.zh + me.zl) % 2 * 2 + me.core]
+    load_hidden.wait()
+    load_projection.wait()
+    proj = jnp.dot(hidden[...], projection[...], preferred_element_type=f32)
+    inverse = lax.rsqrt(jnp.sum(proj * proj, axis=1, keepdims=True) + norm_eps)
+    unit[...] = proj * inverse
+    own_s[...] = (proj * inverse).astype(bf16)
     spread = gather(own_s, column_s, pairs[2], me.b, 64, ends)
     step(spread)
-    for _ in range(5):
-        step(teach, spread)
+    steps(5, teach)
     align = gather(own_s, line_s, pairs[3], me.a, 64, ends, twin)
     step(align)
     for copy in told_by:
         copy.wait_recv()
-    finish(teach, spread)
 
     lane = lax.broadcasted_iota(jnp.int32, (1, 128), 1) // 32 * 128
     tube_at = lax.broadcasted_iota(jnp.int32, (tubes, 128), 0)
@@ -243,23 +297,42 @@
         at = pl.ds(pl.multiple_of(half * 4 * tokens, 128), 4 * tokens)
         parts[at, :] = jnp.dot(picks[half], rows[half], preferred_element_type=f32).astype(bf16)
 
-    weigh(0, 8)
-    step(align)
-    weigh(8, 16)
-    step(align)
-    merge = reduce(parts, me.row_of, land_0, sums_0, pairs[4], me.b, ends, total)
+    half = tokens // 2
+    halves = [dict(off=i * half, n=half) for i in (0, 1)]
+    weigh(0, 5)
+    steps(3, spread)
+    finish(teach)
+    weigh(5, 16)
+    steps(2, spread)
+    steps(3, align)
+    merges = [
+        reduce(parts, me.row_of, land_0, sums_0, pair, me.b, ends, total, **where)
+        for pair, where in zip(pairs[8:10], halves)
+    ]
     add_up((me.zh + 1) % 2)
-    step(merge, align)
+    steps(2, *merges)
     add_up(me.zh)
-    finish(merge, align)
+    step(*merges)
+    steps(2, align)
+    finish(spread)
+    for merge in merges:
+        steps(2, merge)
+    finish(*merges)
     target = total[...]
     own_t[...] = (
         target * lax.rsqrt(jnp.sum(target * target, axis=1, keepdims=True) + norm_eps)
     ).astype(bf16)
 
-    line = gather(own_t, line_t, pairs[5], me.a, 64, ends, twin)
-    column = gather(own_t, column_t, pairs[6], me.b, 64, ends)
-    step(line, column)
+    moves = [
+        (
+            gather(own_t, line_t, pairs[4 + 2 * i], me.a, half // 2, ends, twin, **where),
+            gather(own_t, column_t, pairs[5 + 2 * i], me.b, half // 2, ends, **where),
+        )
+        for i, where in enumerate(halves)
+    ]
+    for move in moves:
+        step(*move)
+    finish(align)
     wide = 256
 
     def student(first, last):
@@ -271,10 +344,14 @@
             )
 
     student(0, 4)
-    for j in range(4, 8):
-        step(line, column)
-        student(j, j + 1)
-    finish(line, column)
+    steps(3, *moves[0])
+    student(4, 6)
+    steps(3, *moves[1])
+    steps(2, *moves[0])
+    student(6, 8)
+    steps(2, *moves[1])
+    finish(*moves[0])
+    finish(*moves[1])
 
     @pl.loop(0, 16 * tokens // wide)
     def _(j):
@@ -291,21 +368,38 @@
     for copy in ends:
         copy.wait_send()
     ends.clear()
-    merge = reduce(
-        parts, lambda d, q: q * 4 + d, land_1, sums_1, pairs[7], me.b, ends, total
-    )
-    pull(2, 4)
-    step(merge)
+    merges = [
+        reduce(parts, lambda d, q: q * 4 + d, land_1, sums_1, pair, me.b, ends, total, **where)
+        for pair, where in zip(pairs[10:12], halves)
+    ]
+    pull(3, 4)
+    step(*merges)
+    pull(2, 3)
+    step(*merges)
     pull(0, 2)
-    finish(merge)
+    step(*merges)
+    for merge in merges:
+        steps(2, merge)
+    finish(*merges)
+    grad_unit = 2.0 * total[...]
+    along = jnp.sum(unit[...] * grad_unit, axis=1, keepdims=True)
+    out[...] = ((grad_unit - unit[...] * along) * inverse).astype(bf16)
     for copy in ends:
         copy.wait_send()
 
 
-def whole(teacher, own, notes):
-    tubes, (tokens, width) = teacher.shape[0], own.shape
-    f32, bf16 = jnp.float32, jnp.bfloat16
+def local(student_hidden, projection, teacher, block_map, block_counts, interp_weights):
+    (tokens, depth), width = student_hidden.shape, projection.shape[1]
+    tubes = teacher.shape[0]
+    f32, bf16, i32 = jnp.float32, jnp.bfloat16, jnp.int32
     buffers = (
+        ((tokens, depth), bf16),
+        ((depth, width), bf16),
+        ((3, 32, 128), i32),
+        ((16, 8, 128), f32),
+        ((tokens, width), f32),
+        ((tokens, width), f32),
+        ((tokens, width), bf16),
         ((16 * tubes, width), bf16),
         ((16, 8, 128), f32),
         ((2, 2048, width), bf16),
@@ -323,48 +417,23 @@
         ((7 * tokens, width), bf16),
         ((3 * tokens, width), bf16),
     )
-    sems = (17, 16, 9, 17, 10, 17, 9, 10)
-    return pl.pallas_call(
+    sems = (17, 16, 9, 17, 17, 9, 17, 9, 10, 10, 10, 10)
+    fields = block_map.reshape(3, -1, 128)
+    kept = pl.BlockSpec(memory_space=pltpu.VMEM)
+    left = pl.BlockSpec(memory_space=pl.ANY)
+    grad_proj = pl.pallas_call(
         whole_kernel,
-        out_shape=jax.ShapeDtypeStruct((tokens, width), f32),
-        in_specs=[pl.BlockSpec(memory_space=pltpu.VMEM)] * 3,
-        out_specs=pl.BlockSpec(memory_space=pltpu.VMEM),
+        out_shape=jax.ShapeDtypeStruct((tokens, width), bf16),
+        in_specs=[left, left, kept, kept, kept, pl.BlockSpec(memory_space=pltpu.SMEM)],
+        out_specs=kept,
         scratch_shapes=[pltpu.VMEM(*b) for b in buffers]
+        + [pltpu.SemaphoreType.DMA((2,))]
         + [pltpu.SemaphoreType.DMA((n,)) for n in sems for _ in (0, 1)],
         compiler_params=pltpu.CompilerParams(
             collective_id=1, has_side_effects=True, vmem_limit_bytes=60 * 2**20
         ),
         name="whole_kernel",
-    )(teacher, own, notes)
-
-
-def notes_of(block_map, block_counts, interp_weights):
-    slots, peers = block_map.shape[2], block_counts.shape[1]
-    per_peer = slots // peers
-    levels = interp_weights.shape[0]
-    fields = block_map[0]
-    matches = fields[2][:, None] == jnp.arange(levels, dtype=jnp.int32)[None, :]
-    weights = jnp.sum(jnp.where(matches, interp_weights[None, :], 0.0), axis=1)
-    live = jnp.arange(per_peer, dtype=jnp.int32)[None, :] < block_counts[0][:, None]
-    scale = weights * live.reshape(slots).astype(jnp.float32)
-    notes = jnp.stack([fields[0].astype(jnp.float32), fields[1].astype(jnp.float32), scale])
-    notes = notes.reshape(3, 2, 4, 4, 2, 2, per_peer)
-    notes = jnp.stack([notes[:, 0], notes[:, 1, :, :, ::-1]], axis=1)
-    notes = notes.transpose(3, 4, 5, 0, 1, 2, 6).reshape(16, 3 * 8 * per_peer // 128, 128)
-    return jnp.pad(notes, ((0, 0), (0, 8 - notes.shape[1]), (0, 0)))
-
-
-def local(student_hidden, projection, teacher, block_map, block_counts, interp_weights):
-    bf16, f32 = jnp.bfloat16, jnp.float32
-    notes = notes_of(block_map, block_counts, interp_weights)
-    proj = jnp.dot(student_hidden, projection, preferred_element_type=f32)
-    inverse = lax.rsqrt(jnp.sum(proj * proj, axis=1, keepdims=True) + norm_eps)
-    unit = proj * inverse
-    student_unit = unit.astype(bf16)
-
-    grad_unit = 2.0 * whole(teacher, student_unit, notes)
-    along = jnp.sum(unit * grad_unit, axis=1, keepdims=True)
-    grad_proj = ((grad_unit - unit * along) * inverse).astype(bf16)
+    )(student_hidden, projection, teacher, fields, block_counts, interp_weights)
     grad_hidden = lax.dot_general(grad_proj, projection, NT, preferred_element_type=f32)
     return grad_hidden.astype(bf16)
 

time: 106 us -> 89.9 us (0.85); the launches traced: 105 us -> 89.8 us
  other arithmetic: 5.61 us -> 0 us
  Pallas kernels: 91.7 us -> 87 us
  local copies, waits for them, and re-layouts: 2.61 us -> 0.01 us
  matrix products: 4.52 us -> 2.77 us
    pallas_call x1, Pallas kernels: 91.7 us -> 87 us  [local(): pl.pallas_call(whole_kernel, out_shape=jax.ShapeDtypeStruct((tokens, widt...]
    reduce_sum x2 -> x0, other arithmetic: 2.08 us -> none  [the longest x1 1.19 us: local(): along = jnp.sum(unit * grad_unit, axis=1, keepdims=True)]
    dot_general x1 -> x0, matrix products: 1.69 us -> none  [local(): proj = jnp.dot(student_hidden, projection, preferred_element_type=f32)]
    convert_element_type x2 -> x0, other arithmetic: 1.6 us -> none  [the longest x1 0.82 us: notes_of(): fields[0].astype(jnp.float32)]
    unnamed x1 -> x0, other arithmetic: 1.57 us -> none
where the time goes in v3:
time: 89.9 us; the launch traced here: 89.8 us
  Pallas kernels  87 us (97%)
  matrix products  2.77 us (3%)
    pallas_call x1, Pallas kernels, local(): pl.pallas_call(whole_kernel, out_shape=jax.ShapeDtypeStruct((tokens, widt...  87 us
    dot_general x1, matrix products, local(): lax.dot_general(grad_proj, projection, NT, preferred_element_type=f32)  2.77 us

profile of v3, /device:TPU:1, one launch (start us, length us, event | category | flops | bytes accessed | tf_op | source)
XLA Modules:
  0.0 89.8 jit_solution(12737505426085182878)
XLA Ops:
  0.0 0.0 copy-start
  0.0 87.0 %whole_kernel.1 = bf16[128,768]{1,0:T(8,128)(2,1)} custom-call(bf16[128,1920]{1,0:T(8,128)(2,1)} %hidden_in.1, bf16[1920,768]{1,0:T(8,128)(2,1)} %projection_in.1, bf16[80,768]{1,0:T(8,128)(2,1)} %teacher.1, s32[3,32,128]{2,1,0:T(8,128)} %bitcast.3, s32[1,128]{1,0:T(1,128)} %block_counts.1, f32[64]{0:T(128)} %interp_weights.1), custom_call_target="tpu_custom_call" | custom-call | tf_op jit(solution)/shard_map/whole_kernel/pallas_call | solution.py:424
  87.0 0.0 copy-done
  87.0 2.8 %convolution_convert_fusion = bf16[128,1920]{1,0:T(8,128)(2,1)} fusion(bf16[128,768]{1,0:T(8,128)(2,1)} %whole_kernel.1, bf16[1920,768]{1,0:T(8,128)(2,1)S(1)} %copy-done), kind=kOutput, calls=%fused_computation | convolution fusion | flops 377733120 | bytes 3637248 | tf_op jit(solution)/shard_map/dot_general | solution.py:437
Async XLA Ops:
  0.0 87.0 %copy-start = (bf16[1920,768]{1,0:T(8,128)(2,1)S(1)}, bf16[1920,768]{1,0:T(8,128)(2,1)}, u32[]{:S(2)}) copy-start(bf16[1920,768]{1,0:T(8,128)(2,1)} %projection_in.1) | copy-start | bytes 8847364

commit v4 on v3

--- a/solution.py
+++ b/solution.py
@@ -147,13 +147,12 @@
     yield
     copies[1].start()
     yield
-    copies[6].start()
-    copies[8].start()
-    yield
     copies[0].wait_recv()
     store(0, 0, n, mine(2, 0), at(land, 0))
     copies[3].start()
     copies[4].start()
+    copies[6].start()
+    copies[8].start()
     yield
     copies[1].wait_recv()
     copies[2].wait_recv()
@@ -267,31 +266,45 @@
     own_s[...] = (proj * inverse).astype(bf16)
     spread = gather(own_s, column_s, pairs[2], me.b, 64, ends)
     step(spread)
-    steps(5, teach)
+    steps(3, teach)
+    for copy in told_by:
+        copy.wait_recv()
+
+    lane = lax.broadcasted_iota(jnp.int32, (1, 128), 1) // 32 * 128
+    tube_at = lax.broadcasted_iota(jnp.int32, (tubes, 256), 0)
+    cell_at = lax.broadcasted_iota(jnp.int32, (4 * tokens, 128), 0)
+
+    @pl.loop(0, 16)
+    def _(s):
+        at = pl.ds(pl.multiple_of(s * 128, 128), 128)
+        note = told[s]
+        for half in (0, 1):
+            cell = note[2 + half : 3 + half].astype(jnp.int32) + lane
+            scale = note[4 + half : 5 + half]
+            picks[half, :, at] = jnp.where(cell_at == cell, scale, 0.0).astype(bf16)
+
+    def weigh(first, last):
+        @pl.loop(first // 4, last // 4)
+        def _(group):
+            for i in range(4):
+                s = group * 4 + i
+                at = pl.ds(pl.multiple_of(s * 128, 128), 128)
+                note = told[s]
+                tube = jnp.concatenate([note[0:1], note[1:2]], axis=1).astype(jnp.int32)
+                select = jnp.where(tube_at == tube, 1.0, 0.0).astype(bf16)
+                chosen = lax.dot_general(
+                    select,
+                    teachers[pl.ds(pl.multiple_of(s * tubes, 16), tubes), :],
+                    (((0,), (0,)), ((), ())),
+                    preferred_element_type=f32,
+                ).astype(bf16)
+                rows[0, at, :] = chosen[:128]
+                rows[1, at, :] = chosen[128:]
+
+    steps(3, spread)
+    steps(2, teach)
     align = gather(own_s, line_s, pairs[3], me.a, 64, ends, twin)
     step(align)
-    for copy in told_by:
-        copy.wait_recv()
-
-    lane = lax.broadcasted_iota(jnp.int32, (1, 128), 1) // 32 * 128
-    tube_at = lax.broadcasted_iota(jnp.int32, (tubes, 128), 0)
-    cell_at = lax.broadcasted_iota(jnp.int32, (4 * tokens, 128), 0)
-
-    def weigh(first, last):
-        @pl.loop(first, last)
-        def _(s):
-            at = pl.ds(pl.multiple_of(s * 128, 128), 128)
-            note = told[s]
-            features = teachers[pl.ds(pl.multiple_of(s * tubes, 16), tubes), :]
-            for half in (0, 1):
-                tube = note[half : half + 1].astype(jnp.int32)
-                cell = note[2 + half : 3 + half].astype(jnp.int32) + lane
-                scale = note[4 + half : 5 + half]
-                select = jnp.where(tube_at == tube, 1.0, 0.0).astype(bf16)
-                rows[half, at, :] = lax.dot_general(
-                    select, features, (((0,), (0,)), ((), ())), preferred_element_type=f32
-                ).astype(bf16)
-                picks[half, :, at] = jnp.where(cell_at == cell, scale, 0.0).astype(bf16)
 
     def add_up(half):
         at = pl.ds(pl.multiple_of(half * 4 * tokens, 128), 4 * tokens)
@@ -299,24 +312,23 @@
 
     half = tokens // 2
     halves = [dict(off=i * half, n=half) for i in (0, 1)]
-    weigh(0, 5)
-    steps(3, spread)
+    weigh(0, 4)
     finish(teach)
-    weigh(5, 16)
-    steps(2, spread)
-    steps(3, align)
+    weigh(4, 16)
     merges = [
         reduce(parts, me.row_of, land_0, sums_0, pair, me.b, ends, total, **where)
         for pair, where in zip(pairs[8:10], halves)
     ]
     add_up((me.zh + 1) % 2)
+    steps(2, spread)
     steps(2, *merges)
+    steps(3, align)
     add_up(me.zh)
-    step(*merges)
     steps(2, align)
     finish(spread)
-    for merge in merges:
-        steps(2, merge)
+    steps(2, merges[0])
+    steps(4, align)
+    steps(2, merges[1])
     finish(*merges)
     target = total[...]
     own_t[...] = (
@@ -350,14 +362,25 @@
     steps(2, *moves[0])
     student(6, 8)
     steps(2, *moves[1])
+
+    def incline(first, last, at_column, columns):
+        some = pl.ds(at_column, columns)
+
+        @pl.loop(first, last)
+        def _(j):
+            at = pl.ds(pl.multiple_of(j * wide, wide), wide)
+            gram_t = lax.dot_general(
+                column_t[some, :], line_t[at, :], NT, preferred_element_type=f32
+            )
+            diff = (gram[some, at] - gram_t) * (1.0 / huber_delta)
+            slope[some, at] = jnp.clip(diff, -1.0, 1.0).astype(bf16)
+
+    early = 5 * tokens
+    incline(0, 2, 0, early)
     finish(*moves[0])
     finish(*moves[1])
-
-    @pl.loop(0, 16 * tokens // wide)
-    def _(j):
-        at = pl.ds(pl.multiple_of(j * wide, wide), wide)
-        gram_t = lax.dot_general(column_t[...], line_t[at, :], NT, preferred_element_type=f32)
-        slope[:, at] = jnp.clip((gram[:, at] - gram_t) * (1.0 / huber_delta), -1.0, 1.0).astype(bf16)
+    incline(0, 2, early, 8 * tokens - early)
+    incline(2, 16 * tokens // wide, 0, 8 * tokens)
 
     def pull(first, last):
         @pl.loop(first, last)
@@ -377,7 +400,6 @@
     pull(2, 3)
     step(*merges)
     pull(0, 2)
-    step(*merges)
     for merge in merges:
         steps(2, merge)
     finish(*merges)

time: 89.9 us -> 88.6 us (0.986)
  Pallas kernels: 87 us -> 85.7 us
    pallas_call x1, Pallas kernels: 87 us -> 85.7 us  [local(): pl.pallas_call(whole_kernel, out_shape=jax.ShapeDtypeStruct((tokens, widt...]
where the time goes in v4:
time: 88.6 us; the launch traced here: 88.5 us
  Pallas kernels  85.7 us (97%)
  matrix products  2.77 us (3%)
    pallas_call x1, Pallas kernels, local(): pl.pallas_call(whole_kernel, out_shape=jax.ShapeDtypeStruct((tokens, widt...  85.7 us
    dot_general x1, matrix products, local(): lax.dot_general(grad_proj, projection, NT, preferred_element_type=f32)  2.77 us

profile of v4, /device:TPU:1, one launch (start us, length us, event | category | flops | bytes accessed | tf_op | source)
XLA Modules:
  0.0 88.5 jit_solution(7724645748646673246)
XLA Ops:
  0.0 0.0 copy-start
  0.0 85.7 %whole_kernel.1 = bf16[128,768]{1,0:T(8,128)(2,1)} custom-call(bf16[128,1920]{1,0:T(8,128)(2,1)} %hidden_in.1, bf16[1920,768]{1,0:T(8,128)(2,1)} %projection_in.1, bf16[80,768]{1,0:T(8,128)(2,1)} %teacher.1, s32[3,32,128]{2,1,0:T(8,128)} %bitcast.3, s32[1,128]{1,0:T(1,128)} %block_counts.1, f32[64]{0:T(128)} %interp_weights.1), custom_call_target="tpu_custom_call" | custom-call | tf_op jit(solution)/shard_map/whole_kernel/pallas_call | solution.py:446
  85.7 0.0 copy-done
  85.7 2.8 %convolution_convert_fusion = bf16[128,1920]{1,0:T(8,128)(2,1)} fusion(bf16[128,768]{1,0:T(8,128)(2,1)} %whole_kernel.1, bf16[1920,768]{1,0:T(8,128)(2,1)S(1)} %copy-done), kind=kOutput, calls=%fused_computation | convolution fusion | flops 377733120 | bytes 3637248 | tf_op jit(solution)/shard_map/dot_general | solution.py:459
Async XLA Ops:
  0.0 85.7 %copy-start = (bf16[1920,768]{1,0:T(8,128)(2,1)S(1)}, bf16[1920,768]{1,0:T(8,128)(2,1)}, u32[]{:S(2)}) copy-start(bf16[1920,768]{1,0:T(8,128)(2,1)} %projection_in.1) | copy-start | bytes 8847364

commit v5 on v4

--- a/solution.py
+++ b/solution.py
@@ -301,10 +301,10 @@
                 rows[0, at, :] = chosen[:128]
                 rows[1, at, :] = chosen[128:]
 
-    steps(3, spread)
     steps(2, teach)
     align = gather(own_s, line_s, pairs[3], me.a, 64, ends, twin)
     step(align)
+    steps(3, spread)
 
     def add_up(half):
         at = pl.ds(pl.multiple_of(half * 4 * tokens, 128), 4 * tokens)
@@ -312,23 +312,22 @@
 
     half = tokens // 2
     halves = [dict(off=i * half, n=half) for i in (0, 1)]
-    weigh(0, 4)
     finish(teach)
-    weigh(4, 16)
+    weigh(0, 16)
+    steps(2, spread)
     merges = [
         reduce(parts, me.row_of, land_0, sums_0, pair, me.b, ends, total, **where)
         for pair, where in zip(pairs[8:10], halves)
     ]
     add_up((me.zh + 1) % 2)
-    steps(2, spread)
     steps(2, *merges)
     steps(3, align)
     add_up(me.zh)
     steps(2, align)
+    steps(2, merges[0])
+    steps(2, merges[1])
+    steps(4, align)
     finish(spread)
-    steps(2, merges[0])
-    steps(4, align)
-    steps(2, merges[1])
     finish(*merges)
     target = total[...]
     own_t[...] = (

time: 88.6 us -> 86.9 us (0.981)
  Pallas kernels: 85.7 us -> 84 us
    pallas_call x1, Pallas kernels: 85.7 us -> 84 us  [local(): pl.pallas_call(whole_kernel, out_shape=jax.ShapeDtypeStruct((tokens, widt...]
where the time goes in v5:
time: 86.9 us; the launch traced here: 86.8 us
  Pallas kernels  84 us (97%)
  matrix products  2.78 us (3%)
    pallas_call x1, Pallas kernels, local(): pl.pallas_call(whole_kernel, out_shape=jax.ShapeDtypeStruct((tokens, widt...  84 us
    dot_general x1, matrix products, local(): lax.dot_general(grad_proj, projection, NT, preferred_element_type=f32)  2.78 us

profile of v5, /device:TPU:1, one launch (start us, length us, event | category | flops | bytes accessed | tf_op | source)
XLA Modules:
  0.0 86.8 jit_solution(16598469524952650039)
XLA Ops:
  0.0 0.0 copy-start
  0.0 84.0 %whole_kernel.1 = bf16[128,768]{1,0:T(8,128)(2,1)} custom-call(bf16[128,1920]{1,0:T(8,128)(2,1)} %hidden_in.1, bf16[1920,768]{1,0:T(8,128)(2,1)} %projection_in.1, bf16[80,768]{1,0:T(8,128)(2,1)} %teacher.1, s32[3,32,128]{2,1,0:T(8,128)} %bitcast.3, s32[1,128]{1,0:T(1,128)} %block_counts.1, f32[64]{0:T(128)} %interp_weights.1), custom_call_target="tpu_custom_call" | custom-call | tf_op jit(solution)/shard_map/whole_kernel/pallas_call | solution.py:445
  84.0 0.0 copy-done
  84.0 2.8 %convolution_convert_fusion = bf16[128,1920]{1,0:T(8,128)(2,1)} fusion(bf16[128,768]{1,0:T(8,128)(2,1)} %whole_kernel.1, bf16[1920,768]{1,0:T(8,128)(2,1)S(1)} %copy-done), kind=kOutput, calls=%fused_computation | convolution fusion | flops 377733120 | bytes 3637248 | tf_op jit(solution)/shard_map/dot_general | solution.py:458
Async XLA Ops:
  0.0 84.0 %copy-start = (bf16[1920,768]{1,0:T(8,128)(2,1)S(1)}, bf16[1920,768]{1,0:T(8,128)(2,1)}, u32[]{:S(2)}) copy-start(bf16[1920,768]{1,0:T(8,128)(2,1)} %projection_in.1) | copy-start | bytes 8847364

commit v6 on v5

--- a/solution.py
+++ b/solution.py
@@ -354,12 +354,11 @@
                 column_s[...], line_s[at, :], NT, preferred_element_type=f32
             )
 
-    student(0, 4)
+    student(0, 6)
     steps(3, *moves[0])
-    student(4, 6)
     steps(3, *moves[1])
+    student(6, 8)
     steps(2, *moves[0])
-    student(6, 8)
     steps(2, *moves[1])
 
     def incline(first, last, at_column, columns):

time: 86.9 us -> 86.9 us (level)
  no operation moved by 1% of the time
where the time goes in v6:
time: 86.9 us; the launch traced here: 86.8 us
  Pallas kernels  84 us (97%)
  matrix products  2.78 us (3%)
    pallas_call x1, Pallas kernels, local(): pl.pallas_call(whole_kernel, out_shape=jax.ShapeDtypeStruct((tokens, widt...  84 us
    dot_general x1, matrix products, local(): lax.dot_general(grad_proj, projection, NT, preferred_element_type=f32)  2.78 us

profile of v6, /device:TPU:1, one launch (start us, length us, event | category | flops | bytes accessed | tf_op | source)
XLA Modules:
  0.0 86.8 jit_solution(72482969237715192)
XLA Ops:
  0.0 0.0 copy-start
  0.0 84.0 %whole_kernel.1 = bf16[128,768]{1,0:T(8,128)(2,1)} custom-call(bf16[128,1920]{1,0:T(8,128)(2,1)} %hidden_in.1, bf16[1920,768]{1,0:T(8,128)(2,1)} %projection_in.1, bf16[80,768]{1,0:T(8,128)(2,1)} %teacher.1, s32[3,32,128]{2,1,0:T(8,128)} %bitcast.3, s32[1,128]{1,0:T(1,128)} %block_counts.1, f32[64]{0:T(128)} %interp_weights.1), custom_call_target="tpu_custom_call" | custom-call | tf_op jit(solution)/shard_map/whole_kernel/pallas_call | solution.py:444
  84.0 0.0 copy-done
  84.0 2.8 %convolution_convert_fusion = bf16[128,1920]{1,0:T(8,128)(2,1)} fusion(bf16[128,768]{1,0:T(8,128)(2,1)} %whole_kernel.1, bf16[1920,768]{1,0:T(8,128)(2,1)S(1)} %copy-done), kind=kOutput, calls=%fused_computation | convolution fusion | flops 377733120 | bytes 3637248 | tf_op jit(solution)/shard_map/dot_general | solution.py:457
Async XLA Ops:
  0.0 84.0 %copy-start = (bf16[1920,768]{1,0:T(8,128)(2,1)S(1)}, bf16[1920,768]{1,0:T(8,128)(2,1)}, u32[]{:S(2)}) copy-start(bf16[1920,768]{1,0:T(8,128)(2,1)} %projection_in.1) | copy-start | bytes 8847364
